TPU v7x, 128 devices: a whole 4x4x4 slice. The times are simulated.
128 devices in a mesh: row: 16 (over z, x), col: 8 (over y, core).
Axes of the slice: x: 4, y: 4, z: 4, core: 2. Of those that a mesh axis runs over, the one named last changes fastest.
Arguments:
- start_block: float32 [8, 131072], P(None, ('row', 'col')), may hold values from -6 to 6
- blocks: bfloat16 [16, 8, 128, 128, 128], P('row', 'col'), as said below
- block_rows: int32 [16, 8, 128], P(None, 'col'), may hold values from 0 to 63, as said below
- block_cols: int32 [16, 8, 128], P(None, 'col'), may hold values from 0 to 127, as said below
- counts: int32 [16, 8], replicated, may hold values from 1 to 128, as said below
Outputs:
- next_block: float32 [8, 131072], P(None, ('row', 'col'))
- tridiagonal: float32 [16, 16], replicated
Inputs may be any that keep to these rules, and one draw needn't show every extreme that they name: `block_rows`: entries of each tile are local block rows below 64; within a tile the used slots name distinct blocks whose global row block is at or after the global column block; slots at or after counts are 0 and not part of H. `block_cols`: local block columns below 128, paired with block_rows; unused slots are 0. `counts`: some tile holds exactly 128 blocks in every draw. Blocks whose global row and column blocks agree are symmetric.
All inputs are finite; a program needn't handle non-finite values.
Results may differ from a plain program's by a relative error of at most 0.0048.
Values may be sent and summed in bfloat16 or wider, within the bound.
A program may use at most 64 MiB of HBM per device.

v0:
```python
import math
import jax
import jax.numpy as jnp
from jax import lax
from jax.sharding import Mesh
from jax.sharding import PartitionSpec as P

ITERS = 2
ROW = ("row_0", "row_1")
COL = ("col_0", "col_1")
ROW_COL = ("row_0", "row_1", "col_0", "col_1")
blocks_per_step = 16


def sent_to_all(value, axis):
    length = lax.axis_size(axis)
    return lax.all_to_all(
        jnp.broadcast_to(value[None], (length, *value.shape)), axis, 0, 0, tiled=True
    )


def joined_along(tiles, dim):
    tiles = jnp.moveaxis(tiles, 0, dim)
    lengths = tiles.shape
    return tiles.reshape(*lengths[:dim], lengths[dim] * lengths[dim + 1], *lengths[dim + 2 :])


def collect(value, axis, dim):
    tiles = sent_to_all(value, axis)
    return joined_along(tiles, dim)


def split_up(value, dim, length):
    lengths = value.shape
    tiles = value.reshape(*lengths[:dim], length, lengths[dim] // length, *lengths[dim + 1 :])
    return jnp.moveaxis(tiles, dim, 0)


def sent_and_summed(value, axis, dim):
    length = lax.axis_size(axis)
    tiles = lax.all_to_all(split_up(value, dim, length), axis, 0, 0, tiled=True)
    return jnp.sum(tiles, axis=0)


def over_axes(value, axes):
    for axis in axes:
        value = lax.psum(value, axis)
    return value


def accumulate(
    stored,
    row_list,
    col_list,
    first_slot,
    live_count,
    tile_row,
    tile_col,
    shape_info,
    row_vector,
    col_vector,
    totals,
):
    row_blocks, col_blocks, piece_blocks, grid_cols = shape_info
    vectors = row_vector.shape[0]
    block_side = stored.shape[-1]
    slot_total = stored.shape[0]
    row_pieces = row_vector.reshape(vectors, row_blocks, block_side)
    col_pieces = col_vector.reshape(vectors, col_blocks, block_side)
    offsets = jnp.arange(blocks_per_step, dtype=jnp.int32)
    row_range = jnp.arange(row_blocks, dtype=jnp.int32)
    col_range = jnp.arange(col_blocks, dtype=jnp.int32)

    def visit(group_index, running):
        row_total, col_total = running
        local_slot = group_index * blocks_per_step + offsets
        is_valid = local_slot < live_count
        slot_ids = jnp.clip(first_slot + local_slot, 0, slot_total - 1)
        tile_data = jnp.take(stored, slot_ids, axis=0)
        row_ids = jnp.take(row_list, slot_ids)
        col_ids = jnp.take(col_list, slot_ids)
        global_row = tile_row * row_blocks + row_ids
        global_col = (
            col_ids // piece_blocks * grid_cols + tile_col
        ) * piece_blocks + col_ids % piece_blocks
        mirror = is_valid & (global_row != global_col)
        col_taken = jnp.take(col_pieces, col_ids, axis=1)
        row_taken = jnp.take(row_pieces, row_ids, axis=1)
        direct = jnp.einsum(
            "gij,kgj->kgi", tile_data, col_taken, preferred_element_type=jnp.float32
        )
        turned = jnp.einsum(
            "gji,kgj->kgi", tile_data, row_taken, preferred_element_type=jnp.float32
        )
        pick_rows = ((row_ids[:, None] == row_range[None, :]) & is_valid[:, None]).astype(
            jnp.float32
        )
        pick_cols = ((col_ids[:, None] == col_range[None, :]) & mirror[:, None]).astype(jnp.float32)
        row_total = row_total + jnp.einsum(
            "gs,kgi->ksi", pick_rows, direct, precision=lax.Precision.HIGHEST
        )
        col_total = col_total + jnp.einsum(
            "gs,kgi->ksi", pick_cols, turned, precision=lax.Precision.HIGHEST
        )
        return (row_total, col_total)

    group_count = (live_count + blocks_per_step - 1) // blocks_per_step
    return lax.fori_loop(0, group_count, visit, totals)


def per_device(start_block, blocks, block_rows, block_cols, counts):
    highest = lax.Precision.HIGHEST
    vectors, piece_len = start_block.shape
    stored = blocks[0, 0]
    block_side = stored.shape[-1]
    grid_rows = lax.axis_size(ROW)
    grid_cols = lax.axis_size(COL)
    piece_blocks = piece_len // block_side
    row_blocks = grid_cols * piece_blocks
    col_blocks = grid_rows * piece_blocks
    shape_info = (row_blocks, col_blocks, piece_blocks, grid_cols)
    tile_row = lax.axis_index(ROW)
    tile_col = lax.axis_index(COL)
    row_lists = block_rows[:, 0, :]
    col_lists = block_cols[:, 0, :]
    own_count = counts[tile_row, tile_col]
    own_rows = row_lists[tile_row]
    own_cols = col_lists[tile_row]
    start_sum = over_axes(jnp.dot(start_block, start_block.T, precision=highest), ROW_COL)
    factor = jnp.linalg.cholesky(start_sum)
    current = lax.linalg.triangular_solve(factor, start_block, left_side=True, lower=True)
    previous = current
    prev_factor = factor
    diagonals = []
    couplings = []
    for step_index in range(ITERS):
        half_block = current.astype(jnp.bfloat16)
        row_vector = collect(half_block, COL, 1)
        col_vector = collect(half_block, ROW, 1)
        row_zero = jnp.zeros((vectors, row_blocks, block_side), jnp.float32)
        col_zero = jnp.zeros((vectors, col_blocks, block_side), jnp.float32)
        row_total, col_total = accumulate(
            stored,
            own_rows,
            own_cols,
            0,
            own_count,
            tile_row,
            tile_col,
            shape_info,
            row_vector,
            col_vector,
            (row_zero, col_zero),
        )
        row_part = sent_and_summed(row_total.reshape(vectors, row_blocks * block_side), COL, 1)
        col_part = sent_and_summed(col_total.reshape(vectors, col_blocks * block_side), ROW, 1)
        image = row_part + col_part
        if step_index > 0:
            image = image - jnp.dot(prev_factor.T, previous, precision=highest)
        local_proj = jnp.dot(current, image.T, precision=highest)
        local_square = jnp.dot(image, image.T, precision=highest)
        projection, squares = (over_axes(local_proj, ROW_COL), over_axes(local_square, ROW_COL))
        image = image - jnp.dot(projection.T, current, precision=highest)
        gram = squares - jnp.dot(projection.T, projection, precision=highest)
        factor = jnp.linalg.cholesky(gram)
        following = lax.linalg.triangular_solve(factor, image, left_side=True, lower=True)
        diagonals.append(projection)
        couplings.append(factor)
        previous, prev_factor, current = (current, factor, following)
    tri_size = ITERS * vectors
    tridiagonal = jnp.zeros((tri_size, tri_size), jnp.float32)
    for step_index in range(ITERS):
        low = step_index * vectors
        tridiagonal = tridiagonal.at[low : low + vectors, low : low + vectors].set(
            diagonals[step_index]
        )
        if step_index + 1 < ITERS:
            tridiagonal = tridiagonal.at[
                low : low + vectors, low + vectors : low + 2 * vectors
            ].set(couplings[step_index])
            tridiagonal = tridiagonal.at[
                low + vectors : low + 2 * vectors, low : low + vectors
            ].set(couplings[step_index].T)
    order_root = math.sqrt(piece_len * grid_rows * grid_cols)
    return (current * order_root, tridiagonal)


def solution(mesh):
    torus = Mesh(mesh.devices.reshape(4, 4, 4, 2), ("row_0", "row_1", "col_0", "col_1"))
    return jax.shard_map(
        per_device,
        mesh=torus,
        in_specs=(
            P(None, ROW_COL),
            P(ROW, COL, None, None, None),
            P(None, COL, None),
            P(None, COL, None),
            P(),
        ),
        out_specs=(P(None, ROW_COL), P()),
        check_vma=False,
    )
```

profile of v0, /device:TPU:1, one launch (start us, length us, event | category | flops | bytes accessed | tf_op | source)
XLA Modules:
  0.0 333.4 jit_solution(16994987881674295431)
XLA Ops:
  0.6 0.7 copy-done
  1.5 10.6 %psum.140 = f32[8,8]{0,1:T(8,128)S(1)} all-reduce(f32[8,8]{0,1:T(8,128)S(1)} %fusion.92), channel_id=1, replica_groups=mesh['row_0'=4,'row_1'=4,'col_0'=4,'col_1'=2] {'row_0'}, use_global_device_ids=true, to_apply=%region_0.0 | all-reduce | flops 64 | bytes 512 | tf_op jit(solution)/shard_map/psum | solution.py:47
  12.1 8.8 %psum.141 = f32[8,8]{0,1:T(8,128)S(1)} all-reduce(f32[8,8]{0,1:T(8,128)S(1)} %psum.140), channel_id=1, replica_groups=mesh['row_0'=4,'row_1'=4,'col_0'=4,'col_1'=2] {'row_1'}, use_global_device_ids=true, to_apply=%region_1.0 | all-reduce | flops 64 | bytes 512 | tf_op jit(solution)/shard_map/psum | solution.py:47
  20.9 8.7 %psum.142 = f32[8,8]{0,1:T(8,128)S(1)} all-reduce(f32[8,8]{0,1:T(8,128)S(1)} %psum.141), channel_id=1, replica_groups=mesh['row_0'=4,'row_1'=4,'col_0'=4,'col_1'=2] {'col_0'}, use_global_device_ids=true, to_apply=%region_2.0 | all-reduce | flops 64 | bytes 512 | tf_op jit(solution)/shard_map/psum | solution.py:47
  29.6 8.6 %psum.143 = f32[8,8]{0,1:T(8,128)S(1)} all-reduce(f32[8,8]{0,1:T(8,128)S(1)} %psum.142), channel_id=1, replica_groups=mesh['row_0'=4,'row_1'=4,'col_0'=4,'col_1'=2] {'col_1'}, use_global_device_ids=true, to_apply=%region_3.0 | all-reduce | flops 64 | bytes 512 | tf_op jit(solution)/shard_map/psum | solution.py:47
  38.2 0.7 cholesky.59
  39.0 0.6 compare_reduce_fusion.2
  39.6 0.6 fusion.66
  40.3 0.6 custom-call.7
  41.2 8.0 %all_to_all.40 = bf16[8,8,1024]{2,1,0:T(8,128)(2,1)S(1)} all-to-all(bf16[8,8,1024]{2,1,0:T(8,128)(2,1)S(1)} %broadcast_in_dim.46), channel_id=1, replica_groups=mesh['row_0'=4,'row_1'=4,'col_0'=4,'col_1'=2] {'col_0','col_1'}, dimensions={0} | all-to-all | bytes 262144 | tf_op jit(solution)/shard_map/all_to_all | solution.py:17
  49.1 0.7 broadcast_in_dim.45
  49.9 3.5 %all-to-all-start = ((bf16[16,8,1024]{2,1,0:T(8,128)(2,1)}), bf16[16,8,1024]{2,1,0:T(8,128)(2,1)S(1)}, u32[]{:S(2)}, u32[]{:S(2)}) async-start(bf16[16,8,1024]{2,1,0:T(8,128)(2,1)} %broadcast_in_dim.45), calls=%async_computation | async-start | bytes 524288 | tf_op jit(solution)/shard_map/all_to_all | solution.py:17
  53.4 1.3 dynamic_slice.9
  55.4 0.7 dynamic-slice_bitcast_fusion
  56.1 5.2 %all-to-all-done = bf16[16,8,1024]{2,1,0:T(8,128)(2,1)S(1)} async-done(((bf16[16,8,1024]{2,1,0:T(8,128)(2,1)}), bf16[16,8,1024]{2,1,0:T(8,128)(2,1)S(1)}, u32[]{:S(2)}, u32[]{:S(2)}) %all-to-all-start) | async-done | bytes 262176 | tf_op jit(solution)/shard_map/all_to_all | solution.py:17
  61.3 8.0 %while.34 = (s32[]{:T(128)}, f32[8,64,128]{2,1,0:T(8,128)S(1)}, f32[8,128,128]{1,2,0:T(8,128)S(1)}, s32[]{:T(128)}, s32[128]{0:T(128)S(1)}, /*index=5*/bf16[8,12...) while((s32[]{:T(128)}, f32[8,64,128]{2,1,0:T(8,128)S(1)}, ...), condition=%wide.region_7.14_spmd.clone, body=%wide.region_6.13_spmd.clone.sunk | while | flops 46901184 | bytes 4142997 | solution.py:108
  61.4 0.7 gather_fusion.2
  62.0 0.7 gather_fusion.1
  62.7 0.7 compare_and_fusion.14
  64.6 2.8 gather_fusion
  68.7 0.7 fusion.142
  69.4 0.9 copy.60
  70.3 5.0 %all-to-all-start.2 = ((f32[8,8,1024]{2,1,0:T(8,128)}), f32[8,8,1024]{2,1,0:T(8,128)S(1)}, u32[]{:S(2)}, u32[]{:S(2)}) async-start(f32[8,8,1024]{2,1,0:T(8,128)} %copy.60), calls=%async_computation.2 | async-start | bytes 524288 | tf_op jit(solution)/shard_map/all_to_all | solution.py:41
  75.6 1.1 copy.62
  76.7 5.1 %all-to-all-done.2 = f32[8,8,1024]{2,1,0:T(8,128)S(1)} async-done(((f32[8,8,1024]{2,1,0:T(8,128)}), f32[8,8,1024]{2,1,0:T(8,128)S(1)}, u32[]{:S(2)}, u32[]{:S(2)}) %all-to-all-start.2) | async-done | bytes 262176 | tf_op jit(solution)/shard_map/all_to_all | solution.py:41
  81.8 58.6 %all-to-all-start.3 = ((f32[16,8,1024]{2,1,0:T(8,128)}), f32[16,8,1024]{2,1,0:T(8,128)S(1)}, u32[]{:S(2)}, u32[]{:S(2)}) async-start(f32[16,8,1024]{2,1,0:T(8,128)} %copy.62), calls=%async_computation.3 | async-start | bytes 1048576 | tf_op jit(solution)/shard_map/all_to_all | solution.py:41
  140.4 0.6 and_reduce_fusion
  141.0 0.6 fusion.89
  141.7 9.1 %all-to-all-done.3 = f32[16,8,1024]{2,1,0:T(8,128)S(1)} async-done(((f32[16,8,1024]{2,1,0:T(8,128)}), f32[16,8,1024]{2,1,0:T(8,128)S(1)}, u32[]{:S(2)}, u32[]{:S(2)}) %all-to-all-start.3) | async-done | bytes 524320 | tf_op jit(solution)/shard_map/all_to_all | solution.py:41
  151.1 6.7 %all-reduce.6 = (f32[8,8]{1,0:T(8,128)S(1)}, f32[8,8]{0,1:T(8,128)S(1)}) all-reduce(f32[8,8]{1,0:T(8,128)S(1)} %fusion.94, f32[8,8]{0,1:T(8,128)S(1)} %fusion.93), channel_id=1, replica_groups=mesh['row_0'=4,'row_1'=4,'col_0'=4,'col_1'=2] {'row_0'}, use_global_device_ids=true, to_apply=%region_14.21 | all-reduce | flops 128 | bytes 1024 | tf_op jit(solution)/shard_map/psum | solution.py:47
  157.9 6.7 %all-reduce.4 = (f32[8,8]{1,0:T(8,128)S(1)}, f32[8,8]{0,1:T(8,128)S(1)}) all-reduce(f32[8,8]{1,0:T(8,128)S(1)} %get-tuple-element.564, f32[8,8]{0,1:T(8,128)S(1)} %get-tuple-element.565), channel_id=1, replica_groups=mesh['row_0'=4,'row_1'=4,'col_0'=4,'col_1'=2] {'row_1'}, use_global_device_ids=true, to_apply=%region_15.22 | all-reduce | flops 128 | bytes 1024 | tf_op jit(solution)/shard_map/psum | solution.py:47
  164.5 7.0 %all-reduce.2 = (f32[8,8]{1,0:T(8,128)S(1)}, f32[8,8]{0,1:T(8,128)S(1)}) all-reduce(f32[8,8]{1,0:T(8,128)S(1)} %get-tuple-element.560, f32[8,8]{0,1:T(8,128)S(1)} %get-tuple-element.561), channel_id=1, replica_groups=mesh['row_0'=4,'row_1'=4,'col_0'=4,'col_1'=2] {'col_0'}, use_global_device_ids=true, to_apply=%region_16.23 | all-reduce | flops 128 | bytes 1024 | tf_op jit(solution)/shard_map/psum | solution.py:47
  171.5 10.3 %all-reduce.8 = (f32[8,8]{1,0:T(8,128)S(1)}, f32[8,8]{0,1:T(8,128)S(1)}) all-reduce(f32[8,8]{1,0:T(8,128)S(1)} %get-tuple-element.556, f32[8,8]{0,1:T(8,128)S(1)} %get-tuple-element.557), channel_id=1, replica_groups=mesh['row_0'=4,'row_1'=4,'col_0'=4,'col_1'=2] {'col_1'}, use_global_device_ids=true, to_apply=%region_17.24 | all-reduce | flops 128 | bytes 1024 | tf_op jit(solution)/shard_map/psum | solution.py:47
  182.4 0.7 cholesky.70
  183.1 0.7 compare_reduce_fusion.1
  183.9 2.6 fusion.83
  186.5 0.6 custom-call.8
  187.3 8.0 %all_to_all.41 = bf16[8,8,1024]{2,1,0:T(8,128)(2,1)S(1)} all-to-all(bf16[8,8,1024]{2,1,0:T(8,128)(2,1)S(1)} %broadcast_in_dim.48), channel_id=1, replica_groups=mesh['row_0'=4,'row_1'=4,'col_0'=4,'col_1'=2] {'col_0','col_1'}, dimensions={0} | all-to-all | bytes 262144 | tf_op jit(solution)/shard_map/all_to_all | solution.py:17
  195.3 0.7 broadcast_in_dim.47
  196.0 3.5 %all-to-all-start.4 = ((bf16[16,8,1024]{2,1,0:T(8,128)(2,1)}), bf16[16,8,1024]{2,1,0:T(8,128)(2,1)S(1)}, u32[]{:S(2)}, u32[]{:S(2)}) async-start(bf16[16,8,1024]{2,1,0:T(8,128)(2,1)} %broadcast_in_dim.47), calls=%async_computation.4 | async-start | bytes 524288 | tf_op jit(solution)/shard_map/all_to_all | solution.py:17
  199.6 7.9 %all-to-all-done.4 = bf16[16,8,1024]{2,1,0:T(8,128)(2,1)S(1)} async-done(((bf16[16,8,1024]{2,1,0:T(8,128)(2,1)}), bf16[16,8,1024]{2,1,0:T(8,128)(2,1)S(1)}, u32[]{:S(2)}, u32[]{:S(2)}) %all-to-all-start.4) | async-done | bytes 262176 | tf_op jit(solution)/shard_map/all_to_all | solution.py:17
  207.5 8.0 %while.35 = (s32[]{:T(128)}, f32[8,64,128]{2,1,0:T(8,128)S(1)}, f32[8,128,128]{1,2,0:T(8,128)S(1)}, s32[]{:T(128)}, s32[128]{0:T(128)S(1)}, /*index=5*/bf16[8,12...) while((s32[]{:T(128)}, f32[8,64,128]{2,1,0:T(8,128)S(1)}, ...), condition=%wide.region_19.26_spmd.clone, body=%wide.region_18.25_spmd.clone.sunk | while | flops 46901184 | bytes 4142997 | solution.py:108
  207.5 0.7 gather_fusion.7
  208.2 0.7 gather_fusion.6
  208.9 0.7 compare_and_fusion.17
  210.8 2.8 gather_fusion.5
  214.8 0.7 fusion.150
  215.6 0.9 copy.67
  216.4 5.0 %all-to-all-start.6 = ((f32[8,8,1024]{2,1,0:T(8,128)}), f32[8,8,1024]{2,1,0:T(8,128)S(1)}, u32[]{:S(2)}, u32[]{:S(2)}) async-start(f32[8,8,1024]{2,1,0:T(8,128)} %copy.67), calls=%async_computation.6 | async-start | bytes 524288 | tf_op jit(solution)/shard_map/all_to_all | solution.py:41
  221.8 1.1 copy.69
  222.9 5.1 %all-to-all-done.6 = f32[8,8,1024]{2,1,0:T(8,128)S(1)} async-done(((f32[8,8,1024]{2,1,0:T(8,128)}), f32[8,8,1024]{2,1,0:T(8,128)S(1)}, u32[]{:S(2)}, u32[]{:S(2)}) %all-to-all-start.6) | async-done | bytes 262176 | tf_op jit(solution)/shard_map/all_to_all | solution.py:41
  228.0 58.6 %all-to-all-start.7 = ((f32[16,8,1024]{2,1,0:T(8,128)}), f32[16,8,1024]{2,1,0:T(8,128)S(1)}, u32[]{:S(2)}, u32[]{:S(2)}) async-start(f32[16,8,1024]{2,1,0:T(8,128)} %copy.69), calls=%async_computation.7 | async-start | bytes 1048576 | tf_op jit(solution)/shard_map/all_to_all | solution.py:41
  286.6 1.8 scatter.15
  288.9 8.0 %all-to-all-done.7 = f32[16,8,1024]{2,1,0:T(8,128)S(1)} async-done(((f32[16,8,1024]{2,1,0:T(8,128)}), f32[16,8,1024]{2,1,0:T(8,128)S(1)}, u32[]{:S(2)}, u32[]{:S(2)}) %all-to-all-start.7) | async-done | bytes 524320 | tf_op jit(solution)/shard_map/all_to_all | solution.py:41
  296.9 0.8 convolution_subtract_fusion.1
  298.1 6.7 %all-reduce.5 = (f32[8,8]{1,0:T(8,128)S(1)}, f32[8,8]{0,1:T(8,128)S(1)}) all-reduce(f32[8,8]{1,0:T(8,128)S(1)} %fusion.96, f32[8,8]{0,1:T(8,128)S(1)} %fusion.95), channel_id=1, replica_groups=mesh['row_0'=4,'row_1'=4,'col_0'=4,'col_1'=2] {'row_0'}, use_global_device_ids=true, to_apply=%region_26.33 | all-reduce | flops 128 | bytes 1024 | tf_op jit(solution)/shard_map/psum | solution.py:47
  304.9 6.7 %all-reduce.3 = (f32[8,8]{1,0:T(8,128)S(1)}, f32[8,8]{0,1:T(8,128)S(1)}) all-reduce(f32[8,8]{1,0:T(8,128)S(1)} %get-tuple-element.562, f32[8,8]{0,1:T(8,128)S(1)} %get-tuple-element.563), channel_id=1, replica_groups=mesh['row_0'=4,'row_1'=4,'col_0'=4,'col_1'=2] {'row_1'}, use_global_device_ids=true, to_apply=%region_27.34 | all-reduce | flops 128 | bytes 1024 | tf_op jit(solution)/shard_map/psum | solution.py:47
  311.6 7.0 %all-reduce.1 = (f32[8,8]{1,0:T(8,128)S(1)}, f32[8,8]{0,1:T(8,128)S(1)}) all-reduce(f32[8,8]{1,0:T(8,128)S(1)} %get-tuple-element.558, f32[8,8]{0,1:T(8,128)S(1)} %get-tuple-element.559), channel_id=1, replica_groups=mesh['row_0'=4,'row_1'=4,'col_0'=4,'col_1'=2] {'col_0'}, use_global_device_ids=true, to_apply=%region_28.35 | all-reduce | flops 128 | bytes 1024 | tf_op jit(solution)/shard_map/psum | solution.py:47
  318.5 10.3 %all-reduce.7 = (f32[8,8]{1,0:T(8,128)S(1)}, f32[8,8]{0,1:T(8,128)S(1)}) all-reduce(f32[8,8]{1,0:T(8,128)S(1)} %get-tuple-element.554, f32[8,8]{0,1:T(8,128)S(1)} %get-tuple-element.555), channel_id=1, replica_groups=mesh['row_0'=4,'row_1'=4,'col_0'=4,'col_1'=2] {'col_1'}, use_global_device_ids=true, to_apply=%region_29.36 | all-reduce | flops 128 | bytes 1024 | tf_op jit(solution)/shard_map/psum | solution.py:47
  329.8 0.7 cholesky.81
  330.6 0.6 compare_reduce_fusion
  331.2 0.6 fusion.67
  331.9 0.6 custom-call.9
  332.5 0.9 convolution_multiply_fusion
  (71 shorter events, 9.1 us)
Async XLA Ops:
  0.6 0.8 copy-start
  49.9 11.4 %all-to-all-start = ((bf16[16,8,1024]{2,1,0:T(8,128)(2,1)}), bf16[16,8,1024]{2,1,0:T(8,128)(2,1)S(1)}, u32[]{:S(2)}, u32[]{:S(2)}) async-start(bf16[16,8,1024]{2,1,0:T(8,128)(2,1)} %broadcast_in_dim.45), calls=%async_computation | async-start | bytes 524288 | tf_op jit(solution)/shard_map/all_to_all | solution.py:17
  70.3 11.5 %all-to-all-start.2 = ((f32[8,8,1024]{2,1,0:T(8,128)}), f32[8,8,1024]{2,1,0:T(8,128)S(1)}, u32[]{:S(2)}, u32[]{:S(2)}) async-start(f32[8,8,1024]{2,1,0:T(8,128)} %copy.60), calls=%async_computation.2 | async-start | bytes 524288 | tf_op jit(solution)/shard_map/all_to_all | solution.py:41
  81.8 69.0 %all-to-all-start.3 = ((f32[16,8,1024]{2,1,0:T(8,128)}), f32[16,8,1024]{2,1,0:T(8,128)S(1)}, u32[]{:S(2)}, u32[]{:S(2)}) async-start(f32[16,8,1024]{2,1,0:T(8,128)} %copy.62), calls=%async_computation.3 | async-start | bytes 1048576 | tf_op jit(solution)/shard_map/all_to_all | solution.py:41
  196.0 11.4 %all-to-all-start.4 = ((bf16[16,8,1024]{2,1,0:T(8,128)(2,1)}), bf16[16,8,1024]{2,1,0:T(8,128)(2,1)S(1)}, u32[]{:S(2)}, u32[]{:S(2)}) async-start(bf16[16,8,1024]{2,1,0:T(8,128)(2,1)} %broadcast_in_dim.47), calls=%async_computation.4 | async-start | bytes 524288 | tf_op jit(solution)/shard_map/all_to_all | solution.py:17
  216.4 11.5 %all-to-all-start.6 = ((f32[8,8,1024]{2,1,0:T(8,128)}), f32[8,8,1024]{2,1,0:T(8,128)S(1)}, u32[]{:S(2)}, u32[]{:S(2)}) async-start(f32[8,8,1024]{2,1,0:T(8,128)} %copy.67), calls=%async_computation.6 | async-start | bytes 524288 | tf_op jit(solution)/shard_map/all_to_all | solution.py:41
  228.0 69.0 %all-to-all-start.7 = ((f32[16,8,1024]{2,1,0:T(8,128)}), f32[16,8,1024]{2,1,0:T(8,128)S(1)}, u32[]{:S(2)}, u32[]{:S(2)}) async-start(f32[16,8,1024]{2,1,0:T(8,128)} %copy.69), calls=%async_computation.7 | async-start | bytes 1048576 | tf_op jit(solution)/shard_map/all_to_all | solution.py:41
  329.7 3.6 %copy-start.1 = (f32[16,16]{1,0:T(8,128)}, f32[16,16]{1,0:T(8,128)S(1)}, u32[]{:S(2)}) copy-start(f32[16,16]{1,0:T(8,128)S(1)} %scatter.19) | copy-start | bytes 3076
where the time goes:
time: 335 us; the launch traced here: 333 us
  starting transfers between devices  134 us (40%)
  blocking collectives  114 us (34%)
  waiting for transfers between devices  40.4 us (12%)
  local copies, waits for them, and re-layouts  23.1 us (7%)
  other arithmetic  12.2 us (4%)
  matrix products  7.58 us (2%)
    all_to_all x4, starting transfers between devices, sent_and_summed(): tiles = lax.all_to_all(split_up(value, dim, length), axis, 0, 0, tiled=True)  127 us
    psum x12, blocking collectives, over_axes(): value = lax.psum(value, axis)  98 us
    all_to_all x4, waiting for transfers between devices, sent_and_summed(): tiles = lax.all_to_all(split_up(value, dim, length), axis, 0, 0, tiled=True)  27.3 us
    all_to_all x2, blocking collectives, sent_to_all(): lax.all_to_all(jnp.broadcast_to(value[None], (length, *value.shape)), axi...  15.9 us
    all_to_all x2, waiting for transfers between devices, sent_to_all(): lax.all_to_all(jnp.broadcast_to(value[None], (length, *value.shape)), axi...  13.1 us
    all_to_all x2, starting transfers between devices, sent_to_all(): lax.all_to_all(jnp.broadcast_to(value[None], (length, *value.shape)), axi...  7.06 us
  transfers between devices with their start and end apart: 6, of which 6 were waited for; matrix products, arithmetic and copies ran while one was open for 2% of the time, Pallas kernels for 0%

commit v1 on v0

--- a/solution.py
+++ b/solution.py
@@ -44,7 +44,8 @@
 
 def over_axes(value, axes):
     for axis in axes:
-        value = lax.psum(value, axis)
+        pieces = lax.all_gather(value, axis)
+        value = jnp.sum(pieces, axis=0)
     return value
 
 

time: 335 us -> 438 us (1.31)
  blocking collectives: 114 us -> 213 us
    all_gather x0 -> x20, blocking collectives: none -> 196 us  [over_axes(): pieces = lax.all_gather(value, axis)]
    psum x12 -> x0, blocking collectives: 98 us -> none  [over_axes(): value = lax.psum(value, axis)]
where the time goes in v1:
time: 438 us; the launch traced here: 436 us
  blocking collectives  213 us (49%)
  starting transfers between devices  138 us (32%)
  waiting for transfers between devices  39.7 us (9%)
  local copies, waits for them, and re-layouts  23.2 us (5%)
  other arithmetic  12.4 us (3%)
  matrix products  7.56 us (2%)
    all_gather x20, blocking collectives, over_axes(): pieces = lax.all_gather(value, axis)  196 us
    all_to_all x4, starting transfers between devices, sent_and_summed(): tiles = lax.all_to_all(split_up(value, dim, length), axis, 0, 0, tiled=True)  128 us
    all_to_all x4, waiting for transfers between devices, sent_and_summed(): tiles = lax.all_to_all(split_up(value, dim, length), axis, 0, 0, tiled=True)  27.3 us
    all_to_all x2, blocking collectives, sent_to_all(): lax.all_to_all(jnp.broadcast_to(value[None], (length, *value.shape)), axi...  17.3 us
    all_to_all x2, waiting for transfers between devices, sent_to_all(): lax.all_to_all(jnp.broadcast_to(value[None], (length, *value.shape)), axi...  12.4 us
    all_to_all x2, starting transfers between devices, sent_to_all(): lax.all_to_all(jnp.broadcast_to(value[None], (length, *value.shape)), axi...  9.31 us
  transfers between devices with their start and end apart: 6, of which 6 were waited for; matrix products, arithmetic and copies ran while one was open for 2% of the time, Pallas kernels for 0%

profile of v1, /device:TPU:1, one launch (start us, length us, event | category | flops | bytes accessed | tf_op | source)
XLA Modules:
  0.0 435.6 jit_solution(1910977513170912685)
XLA Ops:
  0.6 0.7 copy-done
  1.5 11.2 %all-gather = f32[32,8]{1,0:T(8,128)S(1)} all-gather(f32[8,8]{1,0:T(8,128)S(1)} %fusion.92), channel_id=2, replica_groups=mesh['row_0'=4,'row_1'=4,'col_0'=4,'col_1'=2] {'row_0'}, dimensions={0}, use_global_device_ids=true | all-gather | bytes 1280 | tf_op jit(solution)/shard_map/all_gather | solution.py:47
  12.7 9.5 %all-gather.1 = f32[32,8]{1,0:T(8,128)S(1)} all-gather(f32[8,8]{1,0:T(8,128)S(1)} %bitcast_reduce_fusion.14), channel_id=3, replica_groups=mesh['row_0'=4,'row_1'=4,'col_0'=4,'col_1'=2] {'row_1'}, dimensions={0}, use_global_device_ids=true | all-gather | bytes 1280 | tf_op jit(solution)/shard_map/all_gather | solution.py:47
  22.2 9.6 %all-gather.2 = f32[32,8]{1,0:T(8,128)S(1)} all-gather(f32[8,8]{1,0:T(8,128)S(1)} %bitcast_reduce_fusion.13), channel_id=4, replica_groups=mesh['row_0'=4,'row_1'=4,'col_0'=4,'col_1'=2] {'col_0'}, dimensions={0}, use_global_device_ids=true | all-gather | bytes 1280 | tf_op jit(solution)/shard_map/all_gather | solution.py:47
  31.8 10.8 %all-gather.3 = f32[16,8]{1,0:T(8,128)S(1)} all-gather(f32[8,8]{1,0:T(8,128)S(1)} %bitcast_reduce_fusion.12), channel_id=5, replica_groups=mesh['row_0'=4,'row_1'=4,'col_0'=4,'col_1'=2] {'col_1'}, dimensions={0}, use_global_device_ids=true | all-gather | bytes 768 | tf_op jit(solution)/shard_map/all_gather | solution.py:47
  42.7 0.7 cholesky.59
  44.1 0.6 fusion.66
  45.6 9.2 %all_to_all.40 = bf16[8,8,1024]{2,1,0:T(8,128)(2,1)S(1)} all-to-all(bf16[8,8,1024]{2,1,0:T(8,128)(2,1)S(1)} %broadcast_in_dim.46), channel_id=1, replica_groups=mesh['row_0'=4,'row_1'=4,'col_0'=4,'col_1'=2] {'col_0','col_1'}, dimensions={0} | all-to-all | bytes 262144 | tf_op jit(solution)/shard_map/all_to_all | solution.py:17
  54.8 0.7 broadcast_in_dim.45
  55.5 5.8 %all-to-all-start = ((bf16[16,8,1024]{2,1,0:T(8,128)(2,1)}), bf16[16,8,1024]{2,1,0:T(8,128)(2,1)S(1)}, u32[]{:S(2)}, u32[]{:S(2)}) async-start(bf16[16,8,1024]{2,1,0:T(8,128)(2,1)} %broadcast_in_dim.45), calls=%async_computation | async-start | bytes 524288 | tf_op jit(solution)/shard_map/all_to_all | solution.py:17
  61.3 1.3 dynamic_slice.9
  63.3 0.7 dynamic-slice_bitcast_fusion
  64.0 4.9 %all-to-all-done = bf16[16,8,1024]{2,1,0:T(8,128)(2,1)S(1)} async-done(((bf16[16,8,1024]{2,1,0:T(8,128)(2,1)}), bf16[16,8,1024]{2,1,0:T(8,128)(2,1)S(1)}, u32[]{:S(2)}, u32[]{:S(2)}) %all-to-all-start) | async-done | bytes 262176 | tf_op jit(solution)/shard_map/all_to_all | solution.py:17
  69.0 8.0 %while.34 = (s32[]{:T(128)}, f32[8,64,128]{2,1,0:T(8,128)S(1)}, f32[8,128,128]{1,2,0:T(8,128)S(1)}, s32[]{:T(128)}, s32[128]{0:T(128)S(1)}, /*index=5*/bf16[8,12...) while((s32[]{:T(128)}, f32[8,64,128]{2,1,0:T(8,128)S(1)}, ...), condition=%wide.region_7.14_spmd.clone, body=%wide.region_6.13_spmd.clone.sunk | while | flops 46901184 | bytes 4142997 | solution.py:109
  69.0 0.7 gather_fusion.2
  69.7 0.7 gather_fusion.1
  70.3 0.7 compare_and_fusion.14
  72.2 2.8 gather_fusion
  76.3 0.7 fusion.142
  77.0 0.9 copy.84
  77.9 5.6 %all-to-all-start.2 = ((f32[8,8,1024]{2,1,0:T(8,128)}), f32[8,8,1024]{2,1,0:T(8,128)S(1)}, u32[]{:S(2)}, u32[]{:S(2)}) async-start(f32[8,8,1024]{2,1,0:T(8,128)} %copy.84), calls=%async_computation.2 | async-start | bytes 524288 | tf_op jit(solution)/shard_map/all_to_all | solution.py:41
  83.7 1.1 copy.86
  84.8 5.1 %all-to-all-done.2 = f32[8,8,1024]{2,1,0:T(8,128)S(1)} async-done(((f32[8,8,1024]{2,1,0:T(8,128)}), f32[8,8,1024]{2,1,0:T(8,128)S(1)}, u32[]{:S(2)}, u32[]{:S(2)}) %all-to-all-start.2) | async-done | bytes 262176 | tf_op jit(solution)/shard_map/all_to_all | solution.py:41
  89.9 58.6 %all-to-all-start.3 = ((f32[16,8,1024]{2,1,0:T(8,128)}), f32[16,8,1024]{2,1,0:T(8,128)S(1)}, u32[]{:S(2)}, u32[]{:S(2)}) async-start(f32[16,8,1024]{2,1,0:T(8,128)} %copy.86), calls=%async_computation.3 | async-start | bytes 1048576 | tf_op jit(solution)/shard_map/all_to_all | solution.py:41
  149.9 9.1 %all-to-all-done.3 = f32[16,8,1024]{2,1,0:T(8,128)S(1)} async-done(((f32[16,8,1024]{2,1,0:T(8,128)}), f32[16,8,1024]{2,1,0:T(8,128)S(1)}, u32[]{:S(2)}, u32[]{:S(2)}) %all-to-all-start.3) | async-done | bytes 524320 | tf_op jit(solution)/shard_map/all_to_all | solution.py:41
  159.3 9.2 %all-gather.4 = f32[32,8]{1,0:T(8,128)S(1)} all-gather(f32[8,8]{1,0:T(8,128)S(1)} %fusion.93), channel_id=6, replica_groups=mesh['row_0'=4,'row_1'=4,'col_0'=4,'col_1'=2] {'row_0'}, dimensions={0}, use_global_device_ids=true | all-gather | bytes 1280 | tf_op jit(solution)/shard_map/all_gather | solution.py:47
  168.5 9.1 %all-gather.5 = f32[32,8]{1,0:T(8,128)S(1)} all-gather(f32[8,8]{1,0:T(8,128)S(1)} %bitcast_reduce_fusion.11), channel_id=7, replica_groups=mesh['row_0'=4,'row_1'=4,'col_0'=4,'col_1'=2] {'row_1'}, dimensions={0}, use_global_device_ids=true | all-gather | bytes 1280 | tf_op jit(solution)/shard_map/all_gather | solution.py:47
  177.6 9.1 %all-gather.6 = f32[32,8]{1,0:T(8,128)S(1)} all-gather(f32[8,8]{1,0:T(8,128)S(1)} %bitcast_reduce_fusion.10), channel_id=8, replica_groups=mesh['row_0'=4,'row_1'=4,'col_0'=4,'col_1'=2] {'col_0'}, dimensions={0}, use_global_device_ids=true | all-gather | bytes 1280 | tf_op jit(solution)/shard_map/all_gather | solution.py:47
  186.7 12.3 %all-gather.7 = f32[16,8]{1,0:T(8,128)S(1)} all-gather(f32[8,8]{1,0:T(8,128)S(1)} %bitcast_reduce_fusion.9), channel_id=9, replica_groups=mesh['row_0'=4,'row_1'=4,'col_0'=4,'col_1'=2] {'col_1'}, dimensions={0}, use_global_device_ids=true | all-gather | bytes 768 | tf_op jit(solution)/shard_map/all_gather | solution.py:47
  199.1 9.1 %all-gather.8 = f32[32,8]{1,0:T(8,128)S(1)} all-gather(f32[8,8]{1,0:T(8,128)S(1)} %fusion.94), channel_id=10, replica_groups=mesh['row_0'=4,'row_1'=4,'col_0'=4,'col_1'=2] {'row_0'}, dimensions={0}, use_global_device_ids=true | all-gather | bytes 1280 | tf_op jit(solution)/shard_map/all_gather | solution.py:47
  208.2 9.1 %all-gather.9 = f32[32,8]{1,0:T(8,128)S(1)} all-gather(f32[8,8]{1,0:T(8,128)S(1)} %bitcast_reduce_fusion.8), channel_id=11, replica_groups=mesh['row_0'=4,'row_1'=4,'col_0'=4,'col_1'=2] {'row_1'}, dimensions={0}, use_global_device_ids=true | all-gather | bytes 1280 | tf_op jit(solution)/shard_map/all_gather | solution.py:47
  217.3 9.1 %all-gather.10 = f32[32,8]{1,0:T(8,128)S(1)} all-gather(f32[8,8]{1,0:T(8,128)S(1)} %bitcast_reduce_fusion.7), channel_id=12, replica_groups=mesh['row_0'=4,'row_1'=4,'col_0'=4,'col_1'=2] {'col_0'}, dimensions={0}, use_global_device_ids=true | all-gather | bytes 1280 | tf_op jit(solution)/shard_map/all_gather | solution.py:47
  226.5 10.5 %all-gather.11 = f32[16,8]{1,0:T(8,128)S(1)} all-gather(f32[8,8]{1,0:T(8,128)S(1)} %bitcast_reduce_fusion.6), channel_id=13, replica_groups=mesh['row_0'=4,'row_1'=4,'col_0'=4,'col_1'=2] {'col_1'}, dimensions={0}, use_global_device_ids=true | all-gather | bytes 768 | tf_op jit(solution)/shard_map/all_gather | solution.py:47
  237.4 0.7 cholesky.70
  238.2 0.7 compare_reduce_fusion.1
  238.9 2.6 fusion.83
  242.4 8.1 %all_to_all.41 = bf16[8,8,1024]{2,1,0:T(8,128)(2,1)S(1)} all-to-all(bf16[8,8,1024]{2,1,0:T(8,128)(2,1)S(1)} %broadcast_in_dim.48), channel_id=1, replica_groups=mesh['row_0'=4,'row_1'=4,'col_0'=4,'col_1'=2] {'col_0','col_1'}, dimensions={0} | all-to-all | bytes 262144 | tf_op jit(solution)/shard_map/all_to_all | solution.py:17
  250.5 0.7 broadcast_in_dim.47
  251.2 3.5 all-to-all-start.4
  254.8 7.5 %all-to-all-done.4 = bf16[16,8,1024]{2,1,0:T(8,128)(2,1)S(1)} async-done(((bf16[16,8,1024]{2,1,0:T(8,128)(2,1)}), bf16[16,8,1024]{2,1,0:T(8,128)(2,1)S(1)}, u32[]{:S(2)}, u32[]{:S(2)}) %all-to-all-start.4) | async-done | bytes 262176 | tf_op jit(solution)/shard_map/all_to_all | solution.py:17
  262.3 8.0 %while.35 = (s32[]{:T(128)}, f32[8,64,128]{2,1,0:T(8,128)S(1)}, f32[8,128,128]{1,2,0:T(8,128)S(1)}, s32[]{:T(128)}, s32[128]{0:T(128)S(1)}, /*index=5*/bf16[8,12...) while((s32[]{:T(128)}, f32[8,64,128]{2,1,0:T(8,128)S(1)}, ...), condition=%wide.region_19.26_spmd.clone, body=%wide.region_18.25_spmd.clone.sunk | while | flops 46901184 | bytes 4142997 | solution.py:109
  262.4 0.7 gather_fusion.7
  263.0 0.7 gather_fusion.6
  263.7 0.7 compare_and_fusion.17
  265.6 2.8 gather_fusion.5
  269.7 0.7 fusion.150
  270.4 0.9 copy.92
  271.3 5.6 %all-to-all-start.6 = ((f32[8,8,1024]{2,1,0:T(8,128)}), f32[8,8,1024]{2,1,0:T(8,128)S(1)}, u32[]{:S(2)}, u32[]{:S(2)}) async-start(f32[8,8,1024]{2,1,0:T(8,128)} %copy.92), calls=%async_computation.6 | async-start | bytes 524288 | tf_op jit(solution)/shard_map/all_to_all | solution.py:41
  277.1 1.1 copy.94
  278.2 5.1 %all-to-all-done.6 = f32[8,8,1024]{2,1,0:T(8,128)S(1)} async-done(((f32[8,8,1024]{2,1,0:T(8,128)}), f32[8,8,1024]{2,1,0:T(8,128)S(1)}, u32[]{:S(2)}, u32[]{:S(2)}) %all-to-all-start.6) | async-done | bytes 262176 | tf_op jit(solution)/shard_map/all_to_all | solution.py:41
  283.3 58.6 %all-to-all-start.7 = ((f32[16,8,1024]{2,1,0:T(8,128)}), f32[16,8,1024]{2,1,0:T(8,128)S(1)}, u32[]{:S(2)}, u32[]{:S(2)}) async-start(f32[16,8,1024]{2,1,0:T(8,128)} %copy.94), calls=%async_computation.7 | async-start | bytes 1048576 | tf_op jit(solution)/shard_map/all_to_all | solution.py:41
  342.1 1.8 scatter.15
  344.3 8.0 %all-to-all-done.7 = f32[16,8,1024]{2,1,0:T(8,128)S(1)} async-done(((f32[16,8,1024]{2,1,0:T(8,128)}), f32[16,8,1024]{2,1,0:T(8,128)S(1)}, u32[]{:S(2)}, u32[]{:S(2)}) %all-to-all-start.7) | async-done | bytes 524320 | tf_op jit(solution)/shard_map/all_to_all | solution.py:41
  352.4 0.8 convolution_subtract_fusion.1
  353.6 9.2 %all-gather.12 = f32[32,8]{1,0:T(8,128)S(1)} all-gather(f32[8,8]{1,0:T(8,128)S(1)} %fusion.95), channel_id=14, replica_groups=mesh['row_0'=4,'row_1'=4,'col_0'=4,'col_1'=2] {'row_0'}, dimensions={0}, use_global_device_ids=true | all-gather | bytes 1280 | tf_op jit(solution)/shard_map/all_gather | solution.py:47
  362.7 9.1 %all-gather.13 = f32[32,8]{1,0:T(8,128)S(1)} all-gather(f32[8,8]{1,0:T(8,128)S(1)} %bitcast_reduce_fusion.5), channel_id=15, replica_groups=mesh['row_0'=4,'row_1'=4,'col_0'=4,'col_1'=2] {'row_1'}, dimensions={0}, use_global_device_ids=true | all-gather | bytes 1280 | tf_op jit(solution)/shard_map/all_gather | solution.py:47
  371.8 9.1 %all-gather.14 = f32[32,8]{1,0:T(8,128)S(1)} all-gather(f32[8,8]{1,0:T(8,128)S(1)} %bitcast_reduce_fusion.4), channel_id=16, replica_groups=mesh['row_0'=4,'row_1'=4,'col_0'=4,'col_1'=2] {'col_0'}, dimensions={0}, use_global_device_ids=true | all-gather | bytes 1280 | tf_op jit(solution)/shard_map/all_gather | solution.py:47
  381.0 12.3 %all-gather.15 = f32[16,8]{1,0:T(8,128)S(1)} all-gather(f32[8,8]{1,0:T(8,128)S(1)} %bitcast_reduce_fusion.3), channel_id=17, replica_groups=mesh['row_0'=4,'row_1'=4,'col_0'=4,'col_1'=2] {'col_1'}, dimensions={0}, use_global_device_ids=true | all-gather | bytes 768 | tf_op jit(solution)/shard_map/all_gather | solution.py:47
  393.3 9.1 %all-gather.16 = f32[32,8]{1,0:T(8,128)S(1)} all-gather(f32[8,8]{1,0:T(8,128)S(1)} %fusion.96), channel_id=18, replica_groups=mesh['row_0'=4,'row_1'=4,'col_0'=4,'col_1'=2] {'row_0'}, dimensions={0}, use_global_device_ids=true | all-gather | bytes 1280 | tf_op jit(solution)/shard_map/all_gather | solution.py:47
  402.4 9.1 %all-gather.17 = f32[32,8]{1,0:T(8,128)S(1)} all-gather(f32[8,8]{1,0:T(8,128)S(1)} %bitcast_reduce_fusion.2), channel_id=19, replica_groups=mesh['row_0'=4,'row_1'=4,'col_0'=4,'col_1'=2] {'row_1'}, dimensions={0}, use_global_device_ids=true | all-gather | bytes 1280 | tf_op jit(solution)/shard_map/all_gather | solution.py:47
  411.6 9.1 %all-gather.18 = f32[32,8]{1,0:T(8,128)S(1)} all-gather(f32[8,8]{1,0:T(8,128)S(1)} %bitcast_reduce_fusion.1), channel_id=20, replica_groups=mesh['row_0'=4,'row_1'=4,'col_0'=4,'col_1'=2] {'col_0'}, dimensions={0}, use_global_device_ids=true | all-gather | bytes 1280 | tf_op jit(solution)/shard_map/all_gather | solution.py:47
  420.7 10.5 %all-gather.19 = f32[16,8]{1,0:T(8,128)S(1)} all-gather(f32[8,8]{1,0:T(8,128)S(1)} %bitcast_reduce_fusion), channel_id=21, replica_groups=mesh['row_0'=4,'row_1'=4,'col_0'=4,'col_1'=2] {'col_1'}, dimensions={0}, use_global_device_ids=true | all-gather | bytes 768 | tf_op jit(solution)/shard_map/all_gather | solution.py:47
  432.1 0.7 cholesky.81
  434.8 0.9 convolution_multiply_fusion
  (101 shorter events, 14.5 us)
Async XLA Ops:
  0.6 0.8 copy-start
  55.5 13.4 %all-to-all-start = ((bf16[16,8,1024]{2,1,0:T(8,128)(2,1)}), bf16[16,8,1024]{2,1,0:T(8,128)(2,1)S(1)}, u32[]{:S(2)}, u32[]{:S(2)}) async-start(bf16[16,8,1024]{2,1,0:T(8,128)(2,1)} %broadcast_in_dim.45), calls=%async_computation | async-start | bytes 524288 | tf_op jit(solution)/shard_map/all_to_all | solution.py:17
  77.9 12.1 %all-to-all-start.2 = ((f32[8,8,1024]{2,1,0:T(8,128)}), f32[8,8,1024]{2,1,0:T(8,128)S(1)}, u32[]{:S(2)}, u32[]{:S(2)}) async-start(f32[8,8,1024]{2,1,0:T(8,128)} %copy.84), calls=%async_computation.2 | async-start | bytes 524288 | tf_op jit(solution)/shard_map/all_to_all | solution.py:41
  89.9 69.0 %all-to-all-start.3 = ((f32[16,8,1024]{2,1,0:T(8,128)}), f32[16,8,1024]{2,1,0:T(8,128)S(1)}, u32[]{:S(2)}, u32[]{:S(2)}) async-start(f32[16,8,1024]{2,1,0:T(8,128)} %copy.86), calls=%async_computation.3 | async-start | bytes 1048576 | tf_op jit(solution)/shard_map/all_to_all | solution.py:41
  251.2 11.1 %all-to-all-start.4 = ((bf16[16,8,1024]{2,1,0:T(8,128)(2,1)}), bf16[16,8,1024]{2,1,0:T(8,128)(2,1)S(1)}, u32[]{:S(2)}, u32[]{:S(2)}) async-start(bf16[16,8,1024]{2,1,0:T(8,128)(2,1)} %broadcast_in_dim.47), calls=%async_computation.4 | async-start | bytes 524288 | tf_op jit(solution)/shard_map/all_to_all | solution.py:17
  271.3 12.1 %all-to-all-start.6 = ((f32[8,8,1024]{2,1,0:T(8,128)}), f32[8,8,1024]{2,1,0:T(8,128)S(1)}, u32[]{:S(2)}, u32[]{:S(2)}) async-start(f32[8,8,1024]{2,1,0:T(8,128)} %copy.92), calls=%async_computation.6 | async-start | bytes 524288 | tf_op jit(solution)/shard_map/all_to_all | solution.py:41
  283.3 69.0 %all-to-all-start.7 = ((f32[16,8,1024]{2,1,0:T(8,128)}), f32[16,8,1024]{2,1,0:T(8,128)S(1)}, u32[]{:S(2)}, u32[]{:S(2)}) async-start(f32[16,8,1024]{2,1,0:T(8,128)} %copy.94), calls=%async_computation.7 | async-start | bytes 1048576 | tf_op jit(solution)/shard_map/all_to_all | solution.py:41
  432.0 3.6 copy-start.1
